TPU v7x, 256 devices: a whole 4x4x8 slice. The times are simulated.
256 devices in a mesh: section: 4 (over x_hi, core), expert: 64 (over x_lo, z, y).
Axes of the slice: x: 4 (x_hi: 2, x_lo: 2; x = x_hi * 2 + x_lo), y: 4, z: 8, core: 2. Of those that a mesh axis runs over, the one named last changes fastest.
Arguments:
- x_fwd: bfloat16 [4, 8192, 3584], P('section', 'expert'), may hold values from -6 to 6
- routes_fwd: int32 [4, 8192, 2], P('section', 'expert'), may hold values from 0 to 31, all different within a row; in each aligned block of 128 rows (0 to 127, 128 to 255, ..., all dimensions but the last counted through in order) at most 12 rows name the same one
- affinity_fwd: float32 [4, 8192, 2], P('section', 'expert'), may hold values from 0.1 to 1
- x_bwd: bfloat16 [4, 8192, 3584], P('section', 'expert'), may hold values from -6 to 6
- grad_bwd: bfloat16 [4, 8192, 3584], P('section', 'expert'), may hold values from -6 to 6
- routes_bwd: int32 [4, 8192, 2], P('section', 'expert'), may hold values from 0 to 31, all different within a row; in each aligned block of 128 rows (0 to 127, 128 to 255, ..., all dimensions but the last counted through in order) at most 12 rows name the same one
- affinity_bwd: float32 [4, 8192, 2], P('section', 'expert'), may hold values from 0.1 to 1
- up_weight: bfloat16 [4, 3584, 32768], P('section', None, 'expert'), may hold values from -0.09375 to 0.09375
- down_weight: bfloat16 [4, 32768, 3584], P('section', 'expert'), may hold values from -0.1875 to 0.1875
Outputs:
- fwd_next: bfloat16 [4, 8192, 3584], P('section', 'expert')
- bwd_next: bfloat16 [4, 8192, 3584], P('section', 'expert')
Inputs may be any that keep to these rules, and one draw needn't show every extreme that they name: `routes_fwd`: each row names 2 different experts; in each section, among the 128 rows of one device (aligned blocks), no expert is named more than 12 times, a bound that some block reaches. `routes_bwd`: each row names 2 different experts; in each section, among the 128 rows of one device (aligned blocks), no expert is named more than 12 times, a bound that some block reaches.
All inputs are finite; a program needn't handle non-finite values.
Results may differ from a plain program's by a relative error of at most 0.0041.
Values may be sent and summed in bfloat16 or wider, within the bound.
A program may use at most 128 MiB of HBM per device.

v0:
```python
import jax
import jax.numpy as jnp
from jax import lax
from jax.sharding import PartitionSpec as P


def from_partner_2(block, axis, apart):
    count = lax.axis_size(axis)
    route = []
    for low in range(count):
        high = low | 1 << apart
        if high != low and high < count:
            route += [(low, high), (high, low)]
    return lax.ppermute(block, axis, route)


def shifted(shard, axis, by):
    size = lax.axis_size(axis)
    return lax.ppermute(shard, axis, [(i, (i + by) % size) for i in range(size)])


def silu_grad(values):
    sigma = jax.nn.sigmoid(values)
    return sigma * (1.0 + values * (1.0 - sigma))


def slot_table(routes, experts, capacity):
    flat_routes = routes.reshape(-1)
    entries = flat_routes.shape[0]
    onehot = (flat_routes[:, None] == jnp.arange(experts, dtype=jnp.int32)[None, :]).astype(
        jnp.int32
    )
    before = jnp.cumsum(onehot, 0) - onehot
    position = jnp.sum(before * onehot, 1)
    slot_of = flat_routes * capacity + position
    source = (
        jnp.full((experts * capacity,), entries, jnp.int32)
        .at[slot_of]
        .set(jnp.arange(entries, dtype=jnp.int32))
    )
    return (slot_of, source)


def serve_rows(received, up_half, down_half):
    sources = received.shape[0]
    slots = received.shape[2]
    model_width = received.shape[3]
    row_count = sources * slots
    rows_fwd = received[:, 0].reshape(row_count, model_width)
    rows_saved = received[:, 1].reshape(row_count, model_width)
    rows_grad = received[:, 2].reshape(row_count, model_width)
    against_rows = (((1,), (1,)), ((), ()))
    hidden = jax.nn.silu(jnp.dot(rows_fwd, up_half, preferred_element_type=jnp.float32)).astype(
        jnp.bfloat16
    )
    part_fwd = jnp.dot(hidden, down_half, preferred_element_type=jnp.float32).astype(jnp.bfloat16)
    pre_act = jnp.dot(rows_saved, up_half, preferred_element_type=jnp.float32)
    hidden_grad = lax.dot_general(
        rows_grad, down_half, against_rows, preferred_element_type=jnp.float32
    )
    pre_grad = (hidden_grad * silu_grad(pre_act)).astype(jnp.bfloat16)
    part_bwd = lax.dot_general(
        pre_grad, up_half, against_rows, preferred_element_type=jnp.float32
    ).astype(jnp.bfloat16)
    return jnp.stack(
        [
            part_fwd.reshape(sources, slots, model_width),
            part_bwd.reshape(sources, slots, model_width),
        ],
        1,
    )


def combine(inputs, routed_rows, affinity):
    tokens = inputs.shape[0]
    top_count = affinity.shape[1]
    weights = affinity / jnp.sum(affinity, -1, keepdims=True)
    routed = routed_rows.reshape(tokens, top_count, inputs.shape[1]).astype(jnp.float32)
    return (inputs.astype(jnp.float32) + jnp.sum(weights[..., None] * routed, 1)).astype(
        jnp.bfloat16
    )


def per_device(
    x_fwd,
    routes_fwd,
    affinity_fwd,
    x_bwd,
    grad_bwd,
    routes_bwd,
    affinity_bwd,
    up_weight,
    down_weight,
):
    devices = lax.axis_size("expert")
    experts = devices // 2
    tokens = x_fwd.shape[1]
    model_width = x_fwd.shape[2]
    top_count = routes_fwd.shape[2]
    capacity = 3 * tokens * top_count // devices
    half_slots = capacity // 2
    up_half = up_weight[0]
    down_half = down_weight[0]
    slot_fwd, source_fwd = slot_table(routes_fwd[0], experts, capacity)
    slot_bwd, source_bwd = slot_table(routes_bwd[0], experts, capacity)
    zero_row = jnp.zeros((1, model_width), jnp.bfloat16)
    row_table = jnp.concatenate([x_fwd[0], zero_row, x_bwd[0], zero_row, grad_bwd[0], zero_row], 0)
    stride = tokens + 1
    token_fwd = (source_fwd // top_count).reshape(experts, capacity)
    token_bwd = (source_bwd // top_count).reshape(experts, capacity)
    gather_index = jnp.stack([token_fwd, token_bwd + stride, token_bwd + 2 * stride], 1)
    send_index = (
        gather_index.reshape(experts, 3, 2, half_slots)
        .transpose(0, 2, 1, 3)
        .reshape(devices, 3, half_slots)
    )
    outgoing = row_table[send_index]
    received = lax.all_to_all(outgoing, "expert", split_axis=0, concat_axis=0, tiled=True)
    partner = from_partner_2(received, "expert", 0)
    result = serve_rows(jnp.concatenate([received, partner], 2), up_half, down_half)
    piece_slots = received.shape[2]
    from_partner = from_partner_2(result[:, :, piece_slots:], "expert", 0)
    summed = (
        result[:, :, :piece_slots].astype(jnp.float32) + from_partner.astype(jnp.float32)
    ).astype(jnp.bfloat16)
    returned = lax.all_to_all(summed, "expert", split_axis=0, concat_axis=0, tiled=True)
    flat_back = returned.reshape(-1, model_width)

    def back_index(slot_of, member):
        expert_id = slot_of // capacity
        within = slot_of % capacity
        return (
            (2 * expert_id + within // half_slots) * 2 + member
        ) * half_slots + within % half_slots

    index_fwd = back_index(slot_fwd, 0)
    index_bwd = back_index(slot_bwd, 1)
    layer_out = combine(x_fwd[0], flat_back[index_fwd], affinity_fwd[0])
    input_grad = combine(grad_bwd[0], flat_back[index_bwd], affinity_bwd[0])
    fwd_next = shifted(layer_out[None], "section", 1)
    bwd_next = shifted(input_grad[None], "section", -1)
    return (fwd_next, bwd_next)


def solution(mesh):
    in_specs = (
        P("section", "expert", None),
        P("section", "expert", None),
        P("section", "expert", None),
        P("section", "expert", None),
        P("section", "expert", None),
        P("section", "expert", None),
        P("section", "expert", None),
        P("section", None, "expert"),
        P("section", "expert", None),
    )
    out_specs = (P("section", "expert", None), P("section", "expert", None))
    return jax.shard_map(
        per_device, mesh=mesh, in_specs=in_specs, out_specs=out_specs, check_vma=False
    )
```

profile of v0, /device:TPU:1, one launch (start us, length us, event | category | flops | bytes accessed | tf_op | source)
XLA Modules:
  0.0 940.6 jit_solution(5526965452766263269)
XLA Ops:
  10.2 15.5 %concatenate.9 = bf16[387,3584]{1,0:T(8,128)(2,1)S(1)} concatenate(bf16[128,3584]{1,0:T(8,128)(2,1)} %bitcast.85, bf16[1,3584]{1,0:T(2,128)(2,1)S(1)} %broadcast_in_dim.2, bf16[128,3584]{1,0:T(8,128)(2,1)} %bitcast.86, bf16[1,3584]{1,0:T(2,128)(2,1)S(1)} %broadcast_in_dim.2, bf16[128,3584]{1,0:T(8,128)(2,1)} %bitcast.84, bf16[1,3584]{1,0:T(2,128)(2,1)S(1)} %broadcast_in_dim.2), dimensions={0} | concatenate | bytes 5548032 | tf_op jit(solution)/shard_map/concatenate | solution.py:107
  25.8 7.5 gather_fusion
  33.3 13.3 %reshape.417 = bf16[64,3,6,3584]{3,2,1,0:T(8,128)(2,1)} reshape(bf16[1152,3584]{1,0:T(8,128)(2,1)} %gather_fusion) | data formatting | bytes 16515072 | tf_op jit(solution)/shard_map/gather | solution.py:117
  46.6 254.6 %all_to_all.10 = bf16[64,3,6,3584]{3,2,1,0:T(8,128)(2,1)} all-to-all(bf16[64,3,6,3584]{3,2,1,0:T(8,128)(2,1)} %reshape.417), channel_id=1, replica_groups=mesh['section'=4,'expert'=64] {'expert'}, dimensions={0} | all-to-all | bytes 16515072 | tf_op jit(solution)/shard_map/all_to_all | solution.py:118
  301.2 10.0 %copy.72 = bf16[64,3,6,3584]{3,0,2,1:T(8,128)(2,1)} copy(bf16[64,3,6,3584]{3,2,1,0:T(8,128)(2,1)} %all_to_all.10) | data formatting | bytes 16515072 | tf_op jit(solution)/shard_map/all_to_all | solution.py:118
  311.3 177.1 %collective-permute-done = bf16[64,3,6,3584]{3,0,2,1:T(8,128)(2,1)} collective-permute-done((bf16[64,3,6,3584]{3,0,2,1:T(8,128)(2,1)}, bf16[64,3,6,3584]{3,0,2,1:T(8,128)(2,1)}, u32[]{:S(2)}, u32[]{:S(2)}) %collective-permute-start) | collective-permute-done | bytes 8257568 | tf_op jit(solution)/shard_map/ppermute | solution.py:14
  488.4 12.1 %copy.73 = bf16[64,3,6,3584]{3,2,1,0:T(8,128)(2,1)} copy(bf16[64,3,6,3584]{3,0,2,1:T(8,128)(2,1)} %collective-permute-done) | data formatting | bytes 16515072 | tf_op jit(solution)/shard_map/ppermute | solution.py:14
  500.5 15.6 %fusion = (bf16[64,1,12,3584]{3,2,1,0:T(8,128)(2,1)}, bf16[64,1,12,3584]{3,2,1,0:T(8,128)(2,1)}, bf16[64,1,12,3584]{3,2,1,0:T(8,128)(2,1)}) fusion(bf16[64,3,6,3584]{3,2,1,0:T(8,128)(2,1)} %all_to_all.10, bf16[64,3,6,3584]{3,2,1,0:T(8,128)(2,1)} %copy.73), kind=kLoop, calls=%fused_computation.10 | loop fusion | flops 33030144 | bytes 33030144 | tf_op jit(solution)/shard_map/concatenate | solution.py:120
  516.1 9.4 reshape_squeeze.13
  525.5 9.4 reshape_squeeze.12
  549.4 9.3 stack_reshape.11
  558.7 9.4 reshape_squeeze.11
  568.0 7.0 multiply_convert_fusion.1
  579.9 9.6 %stack_reshape.10 = bf16[64,1,12,3584]{3,2,0,1:T(8,128)(2,1)} reshape(bf16[768,3584]{1,0:T(8,128)(2,1)} %convolution_convert_fusion.1) | data formatting | bytes 11010048 | tf_op jit(solution)/shard_map/stack;reshape | solution.py:65
  604.6 117.1 %collective-permute-done.1 = bf16[64,2,6,3584]{3,0,2,1:T(8,128)(2,1)S(1)} collective-permute-done((bf16[64,2,6,3584]{3,0,2,1:T(8,128)(2,1)}, bf16[64,2,6,3584]{3,0,2,1:T(8,128)(2,1)S(1)}, u32[]{:S(2)}, u32[]{:S(2)}) %collective-permute-start.1) | collective-permute-done | bytes 5505056 | tf_op jit(solution)/shard_map/ppermute | solution.py:14
  725.9 11.4 %copy.76 = bf16[64,2,6,3584]{3,1,2,0:T(2,128)(2,1)} copy(bf16[64,2,6,3584]{3,0,2,1:T(8,128)(2,1)S(1)} %add_convert_fusion) | data formatting | bytes 11010048 | tf_op jit(solution)/shard_map/convert_element_type | solution.py:125
  737.3 10.4 %all-to-all-start.1 = ((bf16[64,2,6,3584]{3,1,2,0:T(2,128)(2,1)}), bf16[64,2,6,3584]{3,1,2,0:T(2,128)(2,1)}, u32[]{:S(2)}, u32[]{:S(2)}) async-start(bf16[64,2,6,3584]{3,1,2,0:T(2,128)(2,1)} %copy.76), calls=%async_computation.1 | async-start | bytes 11010048 | tf_op jit(solution)/shard_map/all_to_all | solution.py:126
  748.0 119.8 %all-to-all-done.1 = bf16[64,2,6,3584]{3,1,2,0:T(2,128)(2,1)} async-done(((bf16[64,2,6,3584]{3,1,2,0:T(2,128)(2,1)}), bf16[64,2,6,3584]{3,1,2,0:T(2,128)(2,1)}, u32[]{:S(2)}, u32[]{:S(2)}) %all-to-all-start.1) | async-done | bytes 5505056 | tf_op jit(solution)/shard_map/all_to_all | solution.py:126
  867.8 7.3 copy.77
  875.1 9.7 %reshape.413 = bf16[768,3584]{1,0:T(8,128)(2,1)} reshape(bf16[64,2,6,3584]{3,2,1,0:T(8,128)(2,1)} %copy.77) | data formatting | bytes 11010048 | tf_op jit(solution)/shard_map/reshape | solution.py:127
  884.8 6.8 gather_fusion.2
  895.2 7.3 multiply_reduce_fusion
  916.9 7.3 multiply_reduce_fusion.1
  926.9 10.3 %collective-permute-done.2 = bf16[1,128,3584]{2,1,0:T(8,128)(2,1)S(1)} collective-permute-done((bf16[1,128,3584]{2,1,0:T(8,128)(2,1)S(1)}, bf16[1,128,3584]{2,1,0:T(8,128)(2,1)S(1)}, u32[]{:S(2)}, u32[]{:S(2)}) %collective-permute-start.2) | collective-permute-done | bytes 917536 | tf_op jit(solution)/shard_map/ppermute | solution.py:19
  (96 shorter events, 72.1 us)
Async XLA Ops:
  311.2 177.2 %collective-permute-start = (bf16[64,3,6,3584]{3,0,2,1:T(8,128)(2,1)}, bf16[64,3,6,3584]{3,0,2,1:T(8,128)(2,1)}, u32[]{:S(2)}, u32[]{:S(2)}) collective-permute-start(bf16[64,3,6,3584]{3,0,2,1:T(8,128)(2,1)} %copy.72), channel_id=1, source_target_pairs={{0,1},{1,0},{2,3},{3,2},{4,5},{5,4},{6,7},{7,6},{8,9},{9,8},{10,11... | collective-permute-start | bytes 24772616 | tf_op jit(solution)/shard_map/ppermute | solution.py:14
  534.8 6.2 copy-start.1
  534.8 6.3 copy-start.7
  541.2 3.3 copy-start.6
  568.0 7.0 copy-start.8
  579.9 15.9 %slice-start = ((s8[7340032]{0:T(1024)(128)(4,1)}), s8[3145728]{0:T(1024)(128)(4,1)S(1)}, s32[]{:S(2)}) async-start(s8[7340032]{0:T(1024)(128)(4,1)} %bitcast.82), calls=%async_computation.2 | async-start | bytes 6291456
  589.5 6.3 slice-start.1
  598.8 5.9 copy-start
  604.6 117.1 %collective-permute-start.1 = (bf16[64,2,6,3584]{3,0,2,1:T(8,128)(2,1)}, bf16[64,2,6,3584]{3,0,2,1:T(8,128)(2,1)S(1)}, u32[]{:S(2)}, u32[]{:S(2)}) collective-permute-start(bf16[64,2,6,3584]{3,0,2,1:T(8,128)(2,1)} %slice.59), channel_id=1, source_target_pairs={{0,1},{1,0},{2,3},{3,2},{4,5},{5,4},{6,7},{7,6},{8,9},{9,8},{10,11... | collective-permute-start | bytes 16515080 | tf_op jit(solution)/shard_map/ppermute | solution.py:14
  737.3 10.4 %copy-start.4 = (f32[1,128,2]{1,2,0:T(2,128)S(1)}, f32[1,128,2]{1,2,0:T(2,128)}, u32[]{:S(2)}) copy-start(f32[1,128,2]{1,2,0:T(2,128)} %param.15) | copy-start | bytes 3076
  737.3 10.6 %copy-start.5 = (f32[1,128,2]{1,2,0:T(2,128)S(1)}, f32[1,128,2]{1,2,0:T(2,128)}, u32[]{:S(2)}) copy-start(f32[1,128,2]{1,2,0:T(2,128)} %param.11) | copy-start | bytes 3076
  737.3 130.6 %all-to-all-start.1 = ((bf16[64,2,6,3584]{3,1,2,0:T(2,128)(2,1)}), bf16[64,2,6,3584]{3,1,2,0:T(2,128)(2,1)}, u32[]{:S(2)}, u32[]{:S(2)}) async-start(bf16[64,2,6,3584]{3,1,2,0:T(2,128)(2,1)} %copy.76), calls=%async_computation.1 | async-start | bytes 11010048 | tf_op jit(solution)/shard_map/all_to_all | solution.py:126
  891.6 11.0 %copy-start.2 = (bf16[1,128,3584]{2,1,0:T(8,128)(2,1)S(1)}, bf16[1,128,3584]{2,1,0:T(8,128)(2,1)}, u32[]{:S(2)}) copy-start(bf16[1,128,3584]{2,1,0:T(8,128)(2,1)} %param.13) | copy-start | bytes 2752516
  903.7 23.2 %collective-permute-start.3 = (bf16[1,128,3584]{2,1,0:T(8,128)(2,1)}, bf16[1,128,3584]{2,1,0:T(8,128)(2,1)}, u32[]{:S(2)}, u32[]{:S(2)}) collective-permute-start(bf16[1,128,3584]{2,1,0:T(8,128)(2,1)} %fusion.10), channel_id=1, source_target_pairs={{0,192},{64,0},{128,64},{192,128},{1,193},{65,1},{129,65},{193,129... | collective-permute-start | bytes 2752520 | tf_op jit(solution)/shard_map/ppermute | solution.py:19
  913.2 11.1 %copy-start.3 = (bf16[1,128,3584]{2,1,0:T(8,128)(2,1)S(1)}, bf16[1,128,3584]{2,1,0:T(8,128)(2,1)}, u32[]{:S(2)}) copy-start(bf16[1,128,3584]{2,1,0:T(8,128)(2,1)} %param.9) | copy-start | bytes 2752516
  924.5 12.8 %collective-permute-start.2 = (bf16[1,128,3584]{2,1,0:T(8,128)(2,1)S(1)}, bf16[1,128,3584]{2,1,0:T(8,128)(2,1)S(1)}, u32[]{:S(2)}, u32[]{:S(2)}) collective-permute-start(bf16[1,128,3584]{2,1,0:T(8,128)(2,1)S(1)} %fusion.11), channel_id=1, source_target_pairs={{0,64},{64,128},{128,192},{192,0},{1,65},{65,129},{129,193},{193,1... | collective-permute-start | bytes 2752520 | tf_op jit(solution)/shard_map/ppermute | solution.py:19
where the time goes:
time: 952 us; the launch traced here: 941 us
  waiting for transfers between devices  424 us (45%)
  blocking collectives  255 us (27%)
  local copies, waits for them, and re-layouts  180 us (19%)
  other arithmetic  38.7 us (4%)
  matrix products  26.2 us (3%)
  starting transfers between devices  15.7 us (2%)
    ppermute x2, waiting for transfers between devices, from_partner_2(): return lax.ppermute(block, axis, route)  294 us
    all_to_all x1, blocking collectives, per_device(): lax.all_to_all(outgoing, 'expert', split_axis=0, concat_axis=0, tiled=True)  255 us
    all_to_all x1, waiting for transfers between devices, per_device(): lax.all_to_all(summed, 'expert', split_axis=0, concat_axis=0, tiled=True)  120 us
    another operation x3, local copies, waits for them, and re-layouts, serve_rows(): jnp.stack([part_fwd.reshape(sources, slots, model_width), part_bwd.reshap...  21.9 us
    gather x2, local copies, waits for them, and re-layouts, per_device(): outgoing = row_table[send_index]  20.8 us
  transfers between devices with their start and end apart: 5, of which 4 were waited for; matrix products, arithmetic and copies ran while one was open for 2% of the time, Pallas kernels for 0%

commit v1 on v0

v1 whole, which is shorter than its diff:
```python
import jax
import jax.numpy as jnp
from jax import lax
from jax.sharding import PartitionSpec as P

AGAINST_ROWS = (((1,), (1,)), ((), ()))


def silu_grad(values):
    sigma = jax.nn.sigmoid(values)
    return sigma * (1.0 + values * (1.0 - sigma))


def slots_of(routes, experts, capacity):
    flat = routes.reshape(-1)
    onehot = (flat[:, None] == jnp.arange(experts, dtype=jnp.int32)[None, :]).astype(jnp.int32)
    before = jnp.cumsum(onehot, 0) - onehot
    position = jnp.sum(before * onehot, 1)
    return (flat * capacity + position).reshape(routes.shape)


def pick_matrix(slot_of, slots):
    grid = jnp.arange(slots, dtype=jnp.int32)[:, None, None]
    return jnp.any(grid == slot_of[None, :, :], -1).astype(jnp.bfloat16)


def combine(inputs, results, slot_of, affinity):
    slots = results.shape[0]
    weights = affinity / jnp.sum(affinity, -1, keepdims=True)
    grid = jnp.arange(slots, dtype=jnp.int32)[None, None, :]
    mix = jnp.sum(jnp.where(grid == slot_of[:, :, None], weights[:, :, None], 0.0), 1)
    high = mix.astype(jnp.bfloat16)
    low = (mix - high.astype(jnp.float32)).astype(jnp.bfloat16)
    total = jnp.dot(high, results, preferred_element_type=jnp.float32) + jnp.dot(
        low, results, preferred_element_type=jnp.float32
    )
    return (inputs.astype(jnp.float32) + total).astype(jnp.bfloat16)


def per_device(
    x_fwd, routes_fwd, affinity_fwd, x_bwd, grad_bwd, routes_bwd, affinity_bwd, up_weight, down_weight
):
    devices = lax.axis_size("expert")
    experts = devices // 2
    tokens = x_fwd.shape[1]
    width = x_fwd.shape[2]
    capacity = 3 * tokens * routes_fwd.shape[2] // devices
    slots = experts * capacity
    outer = [(e // 2) * 4 + (0 if e % 2 == 0 else 3) for e in range(experts)]
    inner = [(e // 2) * 4 + (1 if e % 2 == 0 else 2) for e in range(experts)]
    groups = [outer, inner]

    def exchange(block):
        pieces = block.reshape(experts, capacity // 4, 4, width)
        moved = lax.all_to_all(
            pieces, "expert", split_axis=0, concat_axis=0, axis_index_groups=groups, tiled=True
        )
        return moved.reshape(slots, width)

    swap = [(i, i ^ 1) for i in range(devices)]
    up_own, down_own = up_weight[0], down_weight[0]
    up_other = lax.ppermute(up_own, "expert", swap)
    down_other = lax.ppermute(down_own, "expert", swap)

    slot_fwd = slots_of(routes_fwd[0], experts, capacity)
    slot_bwd = slots_of(routes_bwd[0], experts, capacity)
    pick_fwd = pick_matrix(slot_fwd, slots)
    pick_bwd = pick_matrix(slot_bwd, slots)

    def taken(pick, rows):
        return jnp.dot(pick, rows, preferred_element_type=jnp.float32).astype(jnp.bfloat16)

    out_fwd = taken(pick_fwd, x_fwd[0])
    out_x = taken(pick_bwd, x_bwd[0])
    out_g = taken(pick_bwd, grad_bwd[0])
    rows_fwd = exchange(out_fwd)
    rows_x = exchange(out_x)
    rows_g = exchange(out_g)

    def dot(a, b):
        return jnp.dot(a, b, preferred_element_type=jnp.float32)

    def dot_t(a, b):
        return lax.dot_general(a, b, AGAINST_ROWS, preferred_element_type=jnp.float32)

    def forward_half(up, down):
        hidden = jax.nn.silu(dot(rows_fwd, up)).astype(jnp.bfloat16)
        return dot(hidden, down)

    def backward_half(up, down):
        pre = (dot_t(rows_g, down) * silu_grad(dot(rows_x, up))).astype(jnp.bfloat16)
        return dot_t(pre, up)

    done_fwd = (forward_half(up_own, down_own) + forward_half(up_other, down_other)).astype(jnp.bfloat16)
    back_fwd = exchange(done_fwd)
    done_bwd = (backward_half(up_own, down_own) + backward_half(up_other, down_other)).astype(jnp.bfloat16)
    back_bwd = exchange(done_bwd)

    layer_out = combine(x_fwd[0], back_fwd, slot_fwd, affinity_fwd[0])
    input_grad = combine(grad_bwd[0], back_bwd, slot_bwd, affinity_bwd[0])
    sections = lax.axis_size("section")
    fwd_next = lax.ppermute(layer_out[None], "section", [(i, (i + 1) % sections) for i in range(sections)])
    bwd_next = lax.ppermute(input_grad[None], "section", [(i, (i - 1) % sections) for i in range(sections)])
    return (fwd_next, bwd_next)


def solution(mesh):
    rows = P("section", "expert", None)
    return jax.shard_map(
        per_device,
        mesh=mesh,
        in_specs=(rows,) * 7 + (P("section", None, "expert"), rows),
        out_specs=(rows, rows),
        check_vma=False,
    )
```

time: 952 us -> 441 us (0.46)
  blocking collectives: 255 us -> 0 us
  waiting for transfers between devices: 424 us -> 268 us
  local copies, waits for them, and re-layouts: 180 us -> 54.6 us
  matrix products: 26.2 us -> 65.3 us
  other arithmetic: 38.7 us -> 1.99 us
  starting transfers between devices: 15.7 us -> 48.2 us
    all_to_all x1 -> x0, blocking collectives: 255 us -> none  [per_device(): lax.all_to_all(outgoing, 'expert', split_axis=0, concat_axis=0, tiled=True)]
    ppermute x4, waiting for transfers between devices: 305 us -> 73.4 us  [the longest x1 63 us: per_device(): down_other = lax.ppermute(down_own, 'expert', swap)]
    all_to_all x1 -> x5, waiting for transfers between devices: 120 us -> 195 us  [exchange(): lax.all_to_all(pieces, 'expert', split_axis=0, concat_axis=0, axis_index_...]
    another operation x12 -> x3, local copies, waits for them, and re-layouts: 50.3 us -> 0.19 us  [the longest x3 21.9 us: serve_rows(): jnp.stack([part_fwd.reshape(sources, slots, model_width), part_bwd.reshap...]
    reshape x2 -> x10, local copies, waits for them, and re-layouts: 9.7 us -> 49.5 us  [the longest x5 28.1 us: exchange(): pieces = block.reshape(experts, capacity // 4, 4, width)]
    dot_general x5 -> x13, matrix products: 26.2 us -> 65.3 us  [the longest x4 29.7 us: dot(): return jnp.dot(a, b, preferred_element_type=jnp.float32)]
    gather x4 -> x0, local copies, waits for them, and re-layouts: 34.4 us -> none  [the longest x2 20.8 us: per_device(): outgoing = row_table[send_index]]
    all_to_all x1 -> x5, starting transfers between devices: 10.4 us -> 40.9 us  [exchange(): lax.all_to_all(pieces, 'expert', split_axis=0, concat_axis=0, axis_index_...]
  transfers between devices with their start and end apart: 5 -> 9, of which waited for: 4 -> 6; matrix products, arithmetic and copies ran while one was open for 2% -> 25% of each run, Pallas kernels for 0% -> 0%
where the time goes in v1:
time: 441 us; the launch traced here: 439 us
  waiting for transfers between devices  268 us (61%)
  matrix products  65.3 us (15%)
  local copies, waits for them, and re-layouts  54.6 us (12%)
  starting transfers between devices  48.2 us (11%)
    all_to_all x5, waiting for transfers between devices, exchange(): lax.all_to_all(pieces, 'expert', split_axis=0, concat_axis=0, axis_index_...  195 us
    ppermute x1, waiting for transfers between devices, per_device(): down_other = lax.ppermute(down_own, 'expert', swap)  63 us
    all_to_all x5, starting transfers between devices, exchange(): lax.all_to_all(pieces, 'expert', split_axis=0, concat_axis=0, axis_index_...  40.9 us
    dot_general x4, matrix products, dot(): return jnp.dot(a, b, preferred_element_type=jnp.float32)  29.7 us
    reshape x5, local copies, waits for them, and re-layouts, exchange(): pieces = block.reshape(experts, capacity // 4, 4, width)  28.1 us
    reshape x5, local copies, waits for them, and re-layouts, exchange(): return moved.reshape(slots, width)  21.4 us
    dot_general x2, matrix products, dot_t(): lax.dot_general(a, b, AGAINST_ROWS, preferred_element_type=jnp.float32)  18.7 us
    ppermute x1, waiting for transfers between devices, per_device(): lax.ppermute(layer_out[None], 'section', [(i, (i + 1) % sections) for i i...  10.3 us
  transfers between devices with their start and end apart: 9, of which 6 were waited for; matrix products, arithmetic and copies ran while one was open for 25% of the time, Pallas kernels for 0%

profile of v1, /device:TPU:1, one launch (start us, length us, event | category | flops | bytes accessed | tf_op | source)
XLA Modules:
  0.0 439.1 jit_solution(10221248668689824720)
XLA Ops:
  5.5 5.6 %reshape.142 = bf16[32,3,4,3584]{3,2,1,0:T(4,128)(2,1)} reshape(bf16[384,3584]{1,0:T(8,128)(2,1)} %convolution_convert_fusion) | data formatting | bytes 5505024 | tf_op jit(solution)/shard_map/reshape | solution.py:54
  11.1 12.8 %all-to-all-start.3 = ((bf16[32,3,4,3584]{3,2,1,0:T(4,128)(2,1)}), bf16[32,3,4,3584]{3,2,1,0:T(4,128)(2,1)S(1)}, u32[]{:S(2)}, u32[]{:S(2)}) async-start(bf16[32,3,4,3584]{3,2,1,0:T(4,128)(2,1)} %reshape.142), calls=%async_computation.3 | async-start | bytes 5505024 | tf_op jit(solution)/shard_map/all_to_all | solution.py:55
  27.5 5.6 %reshape.140 = bf16[32,3,4,3584]{3,2,1,0:T(4,128)(2,1)} reshape(bf16[384,3584]{1,0:T(8,128)(2,1)} %convolution_convert_fusion.1) | data formatting | bytes 5505024 | tf_op jit(solution)/shard_map/reshape | solution.py:54
  33.1 54.6 %all-to-all-done.3 = bf16[32,3,4,3584]{3,2,1,0:T(4,128)(2,1)S(1)} async-done(((bf16[32,3,4,3584]{3,2,1,0:T(4,128)(2,1)}), bf16[32,3,4,3584]{3,2,1,0:T(4,128)(2,1)S(1)}, u32[]{:S(2)}, u32[]{:S(2)}) %all-to-all-start.3) | async-done | bytes 2752544 | tf_op jit(solution)/shard_map/all_to_all | solution.py:55
  87.7 6.4 %all-to-all-start.2 = ((bf16[32,3,4,3584]{3,2,1,0:T(4,128)(2,1)}), bf16[32,3,4,3584]{3,2,1,0:T(4,128)(2,1)}, u32[]{:S(2)}, u32[]{:S(2)}) async-start(bf16[32,3,4,3584]{3,2,1,0:T(4,128)(2,1)} %reshape.140), calls=%async_computation.2 | async-start | bytes 5505024 | tf_op jit(solution)/shard_map/all_to_all | solution.py:55
  99.4 5.6 %reshape.135 = bf16[32,3,4,3584]{3,2,1,0:T(4,128)(2,1)} reshape(bf16[384,3584]{1,0:T(8,128)(2,1)} %convolution_convert_fusion.2) | data formatting | bytes 5505024 | tf_op jit(solution)/shard_map/reshape | solution.py:54
  105.0 52.9 %all-to-all-done.2 = bf16[32,3,4,3584]{3,2,1,0:T(4,128)(2,1)} async-done(((bf16[32,3,4,3584]{3,2,1,0:T(4,128)(2,1)}), bf16[32,3,4,3584]{3,2,1,0:T(4,128)(2,1)}, u32[]{:S(2)}, u32[]{:S(2)}) %all-to-all-start.2) | async-done | bytes 2752544 | tf_op jit(solution)/shard_map/all_to_all | solution.py:55
  157.9 6.3 %all-to-all-start = ((bf16[32,3,4,3584]{3,2,1,0:T(4,128)(2,1)}), bf16[32,3,4,3584]{3,2,1,0:T(4,128)(2,1)}, u32[]{:S(2)}, u32[]{:S(2)}) async-start(bf16[32,3,4,3584]{3,2,1,0:T(4,128)(2,1)} %reshape.135), calls=%async_computation | async-start | bytes 5505024 | tf_op jit(solution)/shard_map/all_to_all | solution.py:55
  171.0 5.5 %fusion.47 = f32[384,512]{1,0:T(8,128)} fusion(bf16[384,3584]{1,0:T(8,128)(2,1)} %reshape.143, bf16[1,3584,512]{2,1,0:T(8,128)(2,1)} %param.16), kind=kOutput, calls=%fused_computation.81 | convolution fusion | flops 1409286144 | bytes 7208960 | tf_op jit(solution)/shard_map/dot_general | solution.py:81
  181.0 9.0 %fusion.13 = f32[384,3584]{1,0:T(8,128)} fusion(bf16[384,3584]{1,0:T(8,128)(2,1)S(1)} %reshape.141, f32[384,512]{1,0:T(8,128)} %fusion.47, bf16[1,512,3584]{2,1,0:T(8,128)(2,1)} %param.17, bf16[1,3584,512]{2,1,0:T(8,128)(2,1)} %param.16), kind=kOutput, calls=%fused_computation.22 | convolution fusion | flops 2820341760 | bytes 16384000 | tf_op jit(solution)/shard_map/dot_general | solution.py:84
  189.9 63.0 %collective-permute-done.1 = bf16[512,3584]{1,0:T(8,128)(2,1)} collective-permute-done((bf16[512,3584]{1,0:T(8,128)(2,1)}, bf16[512,3584]{1,0:T(8,128)(2,1)}, u32[]{:S(2)}, u32[]{:S(2)}) %collective-permute-start.1) | collective-permute-done | bytes 3670048 | tf_op jit(solution)/shard_map/ppermute | solution.py:63
  253.0 9.7 %fusion.1 = bf16[384,3584]{1,0:T(8,128)(2,1)} fusion(f32[384,3584]{1,0:T(8,128)} %fusion.13, bf16[3584,512]{1,0:T(8,128)(2,1)} %collective-permute-done, bf16[384,3584]{1,0:T(8,128)(2,1)S(1)} %reshape.141, bf16[512,3584]{1,0:T(8,128)(2,1)} %collective-permute-done.1, f32[384,512]{1,0:T(8,128)} %fusion.61), kind=kOutput, calls=%fused_computation.3 | convolution fusion | flops 2823094272 | bytes 19136512 | tf_op jit(solution)/shard_map/dot_general | solution.py:84
  262.7 5.6 %reshape.144 = bf16[32,3,4,3584]{3,2,1,0:T(4,128)(2,1)} reshape(bf16[384,3584]{1,0:T(8,128)(2,1)} %fusion.1) | data formatting | bytes 5505024 | tf_op jit(solution)/shard_map/reshape | solution.py:54
  268.3 9.7 %all-to-all-start.4 = ((bf16[32,3,4,3584]{3,2,1,0:T(4,128)(2,1)}), bf16[32,3,4,3584]{3,2,1,0:T(4,128)(2,1)S(1)}, u32[]{:S(2)}, u32[]{:S(2)}) async-start(bf16[32,3,4,3584]{3,2,1,0:T(4,128)(2,1)} %reshape.144), calls=%async_computation.4 | async-start | bytes 5505024 | tf_op jit(solution)/shard_map/all_to_all | solution.py:55
  278.1 5.4 %reshape.136 = bf16[384,3584]{1,0:T(8,128)(2,1)} reshape(bf16[32,3,4,3584]{3,2,1,0:T(4,128)(2,1)} %all-to-all-done) | data formatting | bytes 5505024 | tf_op jit(solution)/shard_map/reshape | solution.py:58
  283.5 9.5 %fusion.22 = f32[384,3584]{1,0:T(8,128)} fusion(bf16[1,512,3584]{2,1,0:T(8,128)(2,1)} %param.17, bf16[384,3584]{1,0:T(8,128)(2,1)} %reshape.136, bf16[1,3584,512]{2,1,0:T(8,128)(2,1)} %param.16), kind=kOutput, calls=%fused_computation.33 | convolution fusion | flops 2819555328 | bytes 15597568 | tf_op jit(solution)/shard_map/dot_general | solution.py:81
  293.0 10.2 %fusion = bf16[384,3584]{1,0:T(8,128)(2,1)} fusion(f32[384,3584]{1,0:T(8,128)} %fusion.22, bf16[512,3584]{1,0:T(8,128)(2,1)} %collective-permute-done.1, bf16[384,3584]{1,0:T(8,128)(2,1)} %reshape.136, bf16[3584,512]{1,0:T(8,128)(2,1)} %collective-permute-done), kind=kOutput, calls=%fused_computation.2 | convolution fusion | flops 2822307840 | bytes 18350080 | tf_op jit(solution)/shard_map/dot_general | solution.py:81
  303.2 5.6 %reshape.137 = bf16[32,3,4,3584]{3,2,1,0:T(4,128)(2,1)} reshape(bf16[384,3584]{1,0:T(8,128)(2,1)} %fusion) | data formatting | bytes 5505024 | tf_op jit(solution)/shard_map/reshape | solution.py:54
  308.8 32.8 %all-to-all-done.4 = bf16[32,3,4,3584]{3,2,1,0:T(4,128)(2,1)S(1)} async-done(((bf16[32,3,4,3584]{3,2,1,0:T(4,128)(2,1)}), bf16[32,3,4,3584]{3,2,1,0:T(4,128)(2,1)S(1)}, u32[]{:S(2)}, u32[]{:S(2)}) %all-to-all-start.4) | async-done | bytes 2752544 | tf_op jit(solution)/shard_map/all_to_all | solution.py:55
  341.6 5.7 %all-to-all-start.1 = ((bf16[32,3,4,3584]{3,2,1,0:T(4,128)(2,1)}), bf16[32,3,4,3584]{3,2,1,0:T(4,128)(2,1)}, u32[]{:S(2)}, u32[]{:S(2)}) async-start(bf16[32,3,4,3584]{3,2,1,0:T(4,128)(2,1)} %reshape.137), calls=%async_computation.1 | async-start | bytes 5505024 | tf_op jit(solution)/shard_map/all_to_all | solution.py:55
  357.1 54.4 %all-to-all-done.1 = bf16[32,3,4,3584]{3,2,1,0:T(4,128)(2,1)} async-done(((bf16[32,3,4,3584]{3,2,1,0:T(4,128)(2,1)}), bf16[32,3,4,3584]{3,2,1,0:T(4,128)(2,1)}, u32[]{:S(2)}, u32[]{:S(2)}) %all-to-all-start.1) | async-done | bytes 2752544 | tf_op jit(solution)/shard_map/all_to_all | solution.py:55
  411.5 5.4 %reshape.138 = bf16[384,3584]{1,0:T(8,128)(2,1)} reshape(bf16[32,3,4,3584]{3,2,1,0:T(4,128)(2,1)} %all-to-all-done.1) | data formatting | bytes 5505024 | tf_op jit(solution)/shard_map/reshape | solution.py:58
  421.9 4.9 %collective-permute-start.2 = (bf16[1,128,3584]{2,1,0:T(8,128)(2,1)S(1)}, bf16[1,128,3584]{2,1,0:T(8,128)(2,1)S(1)}, u32[]{:S(2)}, u32[]{:S(2)}) collective-permute-start(bf16[1,128,3584]{2,1,0:T(8,128)(2,1)S(1)} %fusion.7), channel_id=1, source_target_pairs={{0,64},{64,128},{128,192},{192,0},{1,65},{65,129},{129,193},{193,1... | collective-permute-start | bytes 2752520 | tf_op jit(solution)/shard_map/ppermute | solution.py:102
  426.9 10.3 %collective-permute-done.2 = bf16[1,128,3584]{2,1,0:T(8,128)(2,1)S(1)} collective-permute-done((bf16[1,128,3584]{2,1,0:T(8,128)(2,1)S(1)}, bf16[1,128,3584]{2,1,0:T(8,128)(2,1)S(1)}, u32[]{:S(2)}, u32[]{:S(2)}) %collective-permute-start.2) | collective-permute-done | bytes 917536 | tf_op jit(solution)/shard_map/ppermute | solution.py:102
  (75 shorter events, 41.5 us)
Async XLA Ops:
  0.6 2.4 copy-start
  11.1 76.6 %all-to-all-start.3 = ((bf16[32,3,4,3584]{3,2,1,0:T(4,128)(2,1)}), bf16[32,3,4,3584]{3,2,1,0:T(4,128)(2,1)S(1)}, u32[]{:S(2)}, u32[]{:S(2)}) async-start(bf16[32,3,4,3584]{3,2,1,0:T(4,128)(2,1)} %reshape.142), calls=%async_computation.3 | async-start | bytes 5505024 | tf_op jit(solution)/shard_map/all_to_all | solution.py:55
  33.1 61.1 %copy-start.8 = (s32[1,128,2]{1,2,0:T(2,128)S(1)}, s32[1,128,2]{1,2,0:T(2,128)}, u32[]{:S(2)}) copy-start(s32[1,128,2]{1,2,0:T(2,128)} %param.10) | copy-start | bytes 3076
  87.7 70.2 %all-to-all-start.2 = ((bf16[32,3,4,3584]{3,2,1,0:T(4,128)(2,1)}), bf16[32,3,4,3584]{3,2,1,0:T(4,128)(2,1)}, u32[]{:S(2)}, u32[]{:S(2)}) async-start(bf16[32,3,4,3584]{3,2,1,0:T(4,128)(2,1)} %reshape.140), calls=%async_computation.2 | async-start | bytes 5505024 | tf_op jit(solution)/shard_map/all_to_all | solution.py:55
  94.1 82.4 %collective-permute-start = (bf16[3584,512]{1,0:T(8,128)(2,1)}, bf16[3584,512]{1,0:T(8,128)(2,1)}, u32[]{:S(2)}, u32[]{:S(2)}) collective-permute-start(bf16[3584,512]{1,0:T(8,128)(2,1)} %bitcast.101), channel_id=1, source_target_pairs={{0,1},{1,0},{2,3},{3,2},{4,5},{5,4},{6,7},{7,6},{8,9},{9,8},{10,11... | collective-permute-start | bytes 11010056 | tf_op jit(solution)/shard_map/ppermute | solution.py:62
  157.9 110.4 %all-to-all-start = ((bf16[32,3,4,3584]{3,2,1,0:T(4,128)(2,1)}), bf16[32,3,4,3584]{3,2,1,0:T(4,128)(2,1)}, u32[]{:S(2)}, u32[]{:S(2)}) async-start(bf16[32,3,4,3584]{3,2,1,0:T(4,128)(2,1)} %reshape.135), calls=%async_computation | async-start | bytes 5505024 | tf_op jit(solution)/shard_map/all_to_all | solution.py:55
  164.2 88.8 %collective-permute-start.1 = (bf16[512,3584]{1,0:T(8,128)(2,1)}, bf16[512,3584]{1,0:T(8,128)(2,1)}, u32[]{:S(2)}, u32[]{:S(2)}) collective-permute-start(bf16[512,3584]{1,0:T(8,128)(2,1)} %bitcast.100), channel_id=1, source_target_pairs={{0,1},{1,0},{2,3},{3,2},{4,5},{5,4},{6,7},{7,6},{8,9},{9,8},{10,11... | collective-permute-start | bytes 11010056 | tf_op jit(solution)/shard_map/ppermute | solution.py:63
  170.9 5.5 %copy-start.5 = (bf16[384,3584]{1,0:T(8,128)(2,1)S(1)}, bf16[384,3584]{1,0:T(8,128)(2,1)}, u32[]{:S(2)}) copy-start(bf16[384,3584]{1,0:T(8,128)(2,1)} %reshape.143) | copy-start | bytes 8257540
  268.3 73.3 %all-to-all-start.4 = ((bf16[32,3,4,3584]{3,2,1,0:T(4,128)(2,1)}), bf16[32,3,4,3584]{3,2,1,0:T(4,128)(2,1)S(1)}, u32[]{:S(2)}, u32[]{:S(2)}) async-start(bf16[32,3,4,3584]{3,2,1,0:T(4,128)(2,1)} %reshape.144), calls=%async_computation.4 | async-start | bytes 5505024 | tf_op jit(solution)/shard_map/all_to_all | solution.py:55
  308.8 39.0 %copy-start.6 = (f32[1,128,2]{1,2,0:T(2,128)S(1)}, f32[1,128,2]{1,2,0:T(2,128)}, u32[]{:S(2)}) copy-start(f32[1,128,2]{1,2,0:T(2,128)} %param.15) | copy-start | bytes 3076
  308.8 39.0 %copy-start.7 = (f32[1,128,2]{1,2,0:T(2,128)S(1)}, f32[1,128,2]{1,2,0:T(2,128)}, u32[]{:S(2)}) copy-start(f32[1,128,2]{1,2,0:T(2,128)} %param.11) | copy-start | bytes 3076
  341.6 6.4 %copy-start.2 = (bf16[32,3,4,3584]{3,2,1,0:T(4,128)(2,1)}, bf16[32,3,4,3584]{3,2,1,0:T(4,128)(2,1)S(1)}, u32[]{:S(2)}) copy-start(bf16[32,3,4,3584]{3,2,1,0:T(4,128)(2,1)S(1)} %all-to-all-done.4) | copy-start | bytes 8257540
  341.6 69.9 %all-to-all-start.1 = ((bf16[32,3,4,3584]{3,2,1,0:T(4,128)(2,1)}), bf16[32,3,4,3584]{3,2,1,0:T(4,128)(2,1)}, u32[]{:S(2)}, u32[]{:S(2)}) async-start(bf16[32,3,4,3584]{3,2,1,0:T(4,128)(2,1)} %reshape.137), calls=%async_computation.1 | async-start | bytes 5505024 | tf_op jit(solution)/shard_map/all_to_all | solution.py:55
  352.3 1.2 copy-start.3
  355.1 71.8 %collective-permute-start.3 = (bf16[1,128,3584]{2,1,0:T(8,128)(2,1)}, bf16[1,128,3584]{2,1,0:T(8,128)(2,1)S(1)}, u32[]{:S(2)}, u32[]{:S(2)}) collective-permute-start(bf16[1,128,3584]{2,1,0:T(8,128)(2,1)} %fusion.6), channel_id=1, source_target_pairs={{0,192},{64,0},{128,64},{192,128},{1,193},{65,1},{129,65},{193,129... | collective-permute-start | bytes 2752520 | tf_op jit(solution)/shard_map/ppermute | solution.py:103
  416.9 2.5 copy-start.4
  419.4 19.7 %copy-start.1 = (bf16[1,128,3584]{2,1,0:T(8,128)(2,1)S(1)}, bf16[1,128,3584]{2,1,0:T(8,128)(2,1)}, u32[]{:S(2)}) copy-start(bf16[1,128,3584]{2,1,0:T(8,128)(2,1)} %param.12) | copy-start | bytes 2752516
  421.9 15.3 %collective-permute-start.2 = (bf16[1,128,3584]{2,1,0:T(8,128)(2,1)S(1)}, bf16[1,128,3584]{2,1,0:T(8,128)(2,1)S(1)}, u32[]{:S(2)}, u32[]{:S(2)}) collective-permute-start(bf16[1,128,3584]{2,1,0:T(8,128)(2,1)S(1)} %fusion.7), channel_id=1, source_target_pairs={{0,64},{64,128},{128,192},{192,0},{1,65},{65,129},{129,193},{193,1... | collective-permute-start | bytes 2752520 | tf_op jit(solution)/shard_map/ppermute | solution.py:102
